TPU v7x, 32 devices: a whole 2x2x4 slice. The times are simulated.
32 devices in a mesh: dp: 8 (over z, y), tensor: 4 (over x, core).
Axes of the slice: x: 2, y: 2, z: 4, core: 2. Of those that a mesh axis runs over, the one named last changes fastest.
Arguments:
- hidden: bfloat16 [128, 4096], P(('dp', 'tensor')), may hold values from -6 to 6
- shortcut: bfloat16 [128, 4096], P('dp'), may hold values from -6 to 6
- expert_ids: int32 [128, 2], P('dp'), may hold values from 0 to 7, all different within a row; in each aligned block of 16 rows (0 to 15, 16 to 31, ...) at most 6 rows name the same one
- route_weight: float32 [128, 2], P('dp'), may hold values from 0.1 to 1
- dense_gain: float32 [4096], replicated, may hold values from 0.5 to 1.5
- moe_gain: float32 [4096], replicated, may hold values from 0.5 to 1.5
- dense_gate: bfloat16 [4096, 8192], P(None, 'dp'), may hold values from -0.09375 to 0.09375
- dense_lift: bfloat16 [4096, 8192], P(None, 'dp'), may hold values from -0.09375 to 0.09375
- dense_down: bfloat16 [8192, 4096], P('dp'), may hold values from -0.0625 to 0.0625
- expert_gate: bfloat16 [4096, 65536], P(None, ('dp', 'tensor')), may hold values from -0.09375 to 0.09375
- expert_lift: bfloat16 [4096, 65536], P(None, ('dp', 'tensor')), may hold values from -0.09375 to 0.09375
- expert_down: bfloat16 [65536, 4096], P(('dp', 'tensor')), may hold values from -0.0625 to 0.0625
Outputs:
- mixed: bfloat16 [128, 4096], P(('dp', 'tensor'))
Inputs may be any that keep to these rules, and one draw needn't show every extreme that they name: `expert_ids`: the 2 experts of a token differ. In each aligned block of 16 rows (the tokens of one index of dp) no expert is named by more than 6 rows, and in every draw some expert is named by exactly 6 rows of some block; every expert is named somewhere.
All inputs are finite; a program needn't handle non-finite values.
Results may differ from a plain program's by a relative error of at most 0.006.
Values may be sent and summed in bfloat16 or wider, within the bound.
A program may use at most 128 MiB of HBM per device.

v0:
```python
import functools

import jax
import jax.numpy as jnp
from jax import lax
from jax.experimental import pallas as pl
from jax.experimental.pallas import tpu as pltpu
from jax.sharding import PartitionSpec as P

E = 8
TOP = 2
CAP = 6
CP = 8
EPSILON = 1e-05
MESH = pl.DeviceIdType.MESH
F32 = jnp.float32
BF16 = jnp.bfloat16


def rms_scale(values):
    return lax.rsqrt(jnp.mean(values * values, axis=-1, keepdims=True) + EPSILON)


def gated(rows, gate, lift):
    g = jnp.dot(rows, gate, preferred_element_type=F32)
    v = jnp.dot(rows, lift, preferred_element_type=F32)
    return (g / (1.0 + jnp.exp(-g)) * v).astype(BF16)


def kernel(
    cfg,
    hidden, shortcut, ids, route, dgain, mgain, dg, dl, dd, eg, el, ed,
    out,
    gpool, lpool, dpool, epool,
    ag, stage, xd, inner_d, ds, dland,
    disp, land, xe, inner_e, rs, rsland, ret, retland, fin, finland,
    gsem, lsem, dsem, esem,
    ag_s, ag_r, di_s, di_r, rl_s, rl_r, ds_s, ds_r, rs_s, rs_r, re_s, re_r, fi_s, fi_r,
):
    np_, nt, cw, ns, nd, ne, dc, ec = cfg
    h, D = hidden.shape
    B = shortcut.shape[0]
    Dq = D // nt
    members = np_ // E
    p = lax.axis_index("dp")
    t = lax.axis_index("tensor")
    nb, nc = D // dc, D // ec
    perq = Dq // ec

    def pair(src_g, src_l, i, q):
        slot = lax.rem(q, ns)
        cols = pl.ds(pl.multiple_of(i * cw, cw), cw)
        return (
            pltpu.make_async_copy(src_g.at[:, cols], gpool.at[slot], gsem.at[slot]),
            pltpu.make_async_copy(src_l.at[:, cols], lpool.at[slot], lsem.at[slot]),
        )

    def down_d(c):
        cols = pl.ds(pl.multiple_of(c * dc, dc), dc)
        return pltpu.make_async_copy(dd.at[:, cols], dpool.at[c], dsem.at[c])

    def quarter(c):
        return lax.rem(t + 1 + c // perq, nt)

    def down_e(c):
        start = quarter(c) * Dq + lax.rem(c, perq) * ec
        cols = pl.ds(pl.multiple_of(start, ec), ec)
        return pltpu.make_async_copy(ed.at[:, cols], epool.at[c], esem.at[c])

    def start_pair(src_g, src_l, i, q):
        for copy in pair(src_g, src_l, i, q):
            copy.start()

    barrier = pltpu.get_barrier_semaphore()

    def greet_dp(k, _):
        pl.semaphore_signal(
            barrier, inc=1, device_id=(lax.rem(p + k, np_), t), device_id_type=MESH
        )
        return 0

    lax.fori_loop(1, np_, greet_dp, 0)
    for j in range(1, nt):
        pl.semaphore_signal(
            barrier, inc=1, device_id=(p, lax.rem(t + j, nt)), device_id_type=MESH
        )

    first = min(ns, nd + ne)
    for q in range(min(first, nd)):
        start_pair(dg, dl, q, q)
    for c in range(nb):
        down_d(c).start()
    for q in range(nd, first):
        start_pair(eg, el, q - nd, q)

    hid = hidden[...].astype(F32)
    ag[p] = (hid * rms_scale(hid) * dgain[...]).astype(BF16)
    pl.semaphore_wait(barrier, np_ + nt - 2)

    def ag_copy(k, src):
        return pltpu.make_async_remote_copy(
            src_ref=ag.at[src], dst_ref=ag.at[src], send_sem=ag_s.at[k],
            recv_sem=ag_r.at[src], device_id=(lax.rem(p + k, np_), t), device_id_type=MESH,
        )

    def send_ag(k, _):
        ag_copy(k, p).start()
        return 0

    lax.fori_loop(1, np_, send_ag, 0)

    wide = 128
    col = lax.broadcasted_iota(jnp.int32, (B, wide), 1)
    col_e = lax.shift_right_logical(col, 3)
    col_s = col & 7
    at0 = jnp.where(ids[:, 0:1] == col_e, 1.0, 0.0).astype(F32)
    at1 = jnp.where(ids[:, 1:2] == col_e, 1.0, 0.0).astype(F32)
    named = at0 + at1
    r_i = lax.broadcasted_iota(jnp.int32, (B, B), 0)
    c_i = lax.broadcasted_iota(jnp.int32, (B, B), 1)
    lower = jnp.where(c_i < r_i, 1.0, 0.0).astype(BF16)
    before = jnp.dot(lower, named.astype(BF16), preferred_element_type=F32)
    spread = jnp.where(before.astype(jnp.int32) == col_s, named, 0.0)
    weighted = spread * (at0 * route[:, 0:1] + at1 * route[:, 1:2])

    sc = rms_scale(shortcut[...].astype(F32))
    mine = pl.ds(pl.multiple_of(t * Dq, Dq), Dq)
    moe_q = (shortcut[:, mine].astype(F32) * sc * mgain[:, mine]).astype(BF16)
    spread_t = jnp.transpose(spread)[: E * CP].astype(BF16)
    buf = jnp.dot(spread_t, moe_q, preferred_element_type=F32)
    disp[...] = buf.reshape(E, CP, Dq).astype(BF16)

    def di_copy(k, src):
        to = lax.rem(p + k, np_)
        return pltpu.make_async_remote_copy(
            src_ref=disp.at[to // members], dst_ref=land.at[t, src], send_sem=di_s.at[k],
            recv_sem=di_r.at[src], device_id=(to, t), device_id_type=MESH,
        )

    def send_di(k, _):
        di_copy(k, p).start()
        return 0

    lax.fori_loop(1, np_, send_di, 0)
    land[t, p] = disp[p // members]

    def recv_ag(k, _):
        ag_copy(k, lax.rem(p + k, np_)).wait_recv()
        return 0

    lax.fori_loop(1, np_, recv_ag, 0)
    for s in range(np_):
        stage[s * h : (s + 1) * h, :] = ag[s].astype(F32)
    xd[...] = stage[...].astype(BF16)

    def dense_step(q, _):
        for copy in pair(dg, dl, q, q):
            copy.wait()
        slot = lax.rem(q, ns)
        cols = pl.ds(pl.multiple_of(q * cw, cw), cw)
        inner_d[:, cols] = gated(xd[...], gpool[slot], lpool[slot])
        later = q + ns - nd

        @pl.when(later < ne)
        def _():
            start_pair(eg, el, later, q + ns)

        return 0

    def rl_copy(j, src):
        return pltpu.make_async_remote_copy(
            src_ref=land.at[src], dst_ref=land.at[src], send_sem=rl_s.at[j],
            recv_sem=rl_r.at[src], device_id=(p, lax.rem(t + j, nt)), device_id_type=MESH,
        )

    half = nd // 2
    lax.fori_loop(0, half, dense_step, 0)

    def recv_di(k, _):
        di_copy(k, lax.rem(p + k, np_)).wait_recv()
        return 0

    lax.fori_loop(1, np_, recv_di, 0)
    for j in range(1, nt):
        rl_copy(j, t).start()
    lax.fori_loop(half, nd, dense_step, 0)

    def dense_down_step(c, _):
        down_d(c).wait()
        o = jnp.dot(inner_d[...], dpool[c], preferred_element_type=F32)
        cols = pl.ds(pl.multiple_of(c * dc, dc), dc)
        for s in range(np_):
            ds[s, :, cols] = o[s * h : (s + 1) * h, :].astype(BF16)
        return 0

    lax.fori_loop(0, nb, dense_down_step, 0)

    def ds_copy(k, src):
        to = lax.rem(p + k, np_)
        return pltpu.make_async_remote_copy(
            src_ref=ds.at[to], dst_ref=dland.at[src], send_sem=ds_s.at[k],
            recv_sem=ds_r.at[src], device_id=(to, t), device_id_type=MESH,
        )

    def send_ds(k, _):
        ds_copy(k, p).start()
        return 0

    lax.fori_loop(1, np_, send_ds, 0)

    for j in range(1, nt):
        rl_copy(j, lax.rem(t + j, nt)).wait_recv()
    for q in range(nt):
        xe[:, q * Dq : (q + 1) * Dq] = land[q].astype(F32).reshape(np_ * CP, Dq).astype(BF16)

    def expert_step(i, _):
        q = i + nd
        for copy in pair(eg, el, i, q):
            copy.wait()
        slot = lax.rem(q, ns)
        cols = pl.ds(pl.multiple_of(i * cw, cw), cw)
        inner_e[:, cols] = gated(xe[...], gpool[slot], lpool[slot])

        @pl.when(i + ns < ne)
        def _():
            start_pair(eg, el, i + ns, q + ns)

        return 0

    tail = min(max(ne - ns, 0), ne)
    lax.fori_loop(0, tail, expert_step, 0)
    for c in range(nc):
        down_e(c).start()
    lax.fori_loop(tail, ne, expert_step, 0)

    def rs_copy(j, to, src):
        return pltpu.make_async_remote_copy(
            src_ref=rs.at[to], dst_ref=rsland.at[src], send_sem=rs_s.at[j],
            recv_sem=rs_r.at[src], device_id=(p, lax.rem(t + j, nt)), device_id_type=MESH,
        )

    def expert_down_step(c, _):
        down_e(c).wait()
        o = jnp.dot(inner_e[...], epool[c], preferred_element_type=F32)
        cols = pl.ds(pl.multiple_of(lax.rem(c, perq) * ec, ec), ec)
        rs[quarter(c), :, :, cols] = o.reshape(np_, CP, ec).astype(BF16)
        j = c // perq + 1

        @pl.when((lax.rem(c, perq) == perq - 1) & (j < nt))
        def _():
            rs_copy(j, lax.rem(t + j, nt), t).start()

        return 0

    lax.fori_loop(0, nc, expert_down_step, 0)

    total = rs[t].astype(F32)
    for j in range(1, nt):
        src = lax.rem(t + j, nt)
        rs_copy(j, src, src).wait_recv()
        total = total + rsland[src].astype(F32)
    ret[...] = total.astype(BF16)

    def re_copy(k, src):
        to = lax.rem(p + k, np_)
        return pltpu.make_async_remote_copy(
            src_ref=ret.at[to], dst_ref=retland.at[src], send_sem=re_s.at[k],
            recv_sem=re_r.at[src], device_id=(to, t), device_id_type=MESH,
        )

    def send_re(k, _):
        re_copy(k, p).start()
        return 0

    lax.fori_loop(1, np_, send_re, 0)
    retland[p] = ret[p]

    dland[p] = ds[p]

    def recv_ds(k, _):
        ds_copy(k, lax.rem(p + k, np_)).wait_recv()
        return 0

    lax.fori_loop(1, np_, recv_ds, 0)
    acc = hid
    for s in range(np_):
        acc = acc + dland[s].astype(F32)

    def recv_re(k, _):
        re_copy(k, lax.rem(p + k, np_)).wait_recv()
        return 0

    lax.fori_loop(1, np_, recv_re, 0)
    summed = jnp.sum(retland[...].astype(F32).reshape(E, members, CP, Dq), axis=1)
    moe = jnp.dot(
        weighted[:, : E * CP], summed.reshape(E * CP, Dq),
        precision=lax.Precision.HIGHEST, preferred_element_type=F32,
    )
    for q in range(nt):
        fin[q] = moe[q * h : (q + 1) * h, :]

    def fi_copy(j, src):
        to = lax.rem(t + j, nt)
        return pltpu.make_async_remote_copy(
            src_ref=fin.at[to], dst_ref=finland.at[src], send_sem=fi_s.at[j],
            recv_sem=fi_r.at[src], device_id=(p, to), device_id_type=MESH,
        )

    for j in range(1, nt):
        fi_copy(j, t).start()
    finland[t] = fin[t]
    for j in range(1, nt):
        fi_copy(j, lax.rem(t + j, nt)).wait_recv()
    for q in range(nt):
        cols = slice(q * Dq, (q + 1) * Dq)
        out[:, cols] = (acc[:, cols] + finland[q]).astype(BF16)

    def sent(k, _):
        ag_copy(k, p).wait_send()
        di_copy(k, p).wait_send()
        ds_copy(k, p).wait_send()
        re_copy(k, p).wait_send()
        return 0

    lax.fori_loop(1, np_, sent, 0)
    for j in range(1, nt):
        rl_copy(j, t).wait_send()
        rs_copy(j, lax.rem(t + j, nt), t).wait_send()
        fi_copy(j, t).wait_send()


def local(np_, nt, hidden, shortcut, ids, route, dgain, mgain, dg, dl, dd, eg, el, ed):
    h, D = hidden.shape
    Dq = D // nt
    fd, fe = dg.shape[1], eg.shape[1]
    cw = min(256, fd, fe)
    nd, ne = fd // cw, fe // cw
    ns = min(6, nd + ne)
    dc, ec = min(1024, D), min(512, Dq)
    cfg = (np_, nt, cw, ns, nd, ne, dc, ec)
    dma = pltpu.SemaphoreType.DMA
    vm = pltpu.VMEM
    vspec = pl.BlockSpec(memory_space=pltpu.VMEM)
    aspec = pl.BlockSpec(memory_space=pl.ANY)
    return pl.pallas_call(
        functools.partial(kernel, cfg),
        out_shape=jax.ShapeDtypeStruct((h, D), BF16),
        in_specs=[vspec] * 6 + [aspec] * 6,
        out_specs=vspec,
        scratch_shapes=[
            vm((ns, D, cw), BF16), vm((ns, D, cw), BF16),
            vm((D // dc, fd, dc), BF16), vm((D // ec, fe, ec), BF16),
            vm((np_, h, D), BF16), vm((np_ * h, D), F32), vm((np_ * h, D), BF16),
            vm((np_ * h, fd), BF16), vm((np_, h, D), BF16), vm((np_, h, D), BF16),
            vm((E, CP, Dq), BF16), vm((nt, np_, CP, Dq), BF16), vm((np_ * CP, D), BF16),
            vm((np_ * CP, fe), BF16), vm((nt, np_, CP, Dq), BF16), vm((nt, np_, CP, Dq), BF16),
            vm((np_, CP, Dq), BF16), vm((np_, CP, Dq), BF16),
            vm((nt, h, Dq), F32), vm((nt, h, Dq), F32),
            dma((ns,)), dma((ns,)), dma((D // dc,)), dma((D // ec,)),
            dma((np_,)), dma((np_,)), dma((np_,)), dma((np_,)),
            dma((nt,)), dma((nt,)), dma((np_,)), dma((np_,)),
            dma((nt,)), dma((nt,)), dma((np_,)), dma((np_,)),
            dma((nt,)), dma((nt,)),
        ],
        compiler_params=pltpu.CompilerParams(
            collective_id=0, has_side_effects=True, vmem_limit_bytes=64 * 1024 * 1024 - 65536
        ),
    )(hidden, shortcut, ids, route, dgain.reshape(1, D), mgain.reshape(1, D), dg, dl, dd, eg, el, ed)


def solution(mesh):
    in_specs = (
        P(("dp", "tensor"), None),
        P("dp", None),
        P("dp", None),
        P("dp", None),
        P(),
        P(),
        P(None, "dp"),
        P(None, "dp"),
        P("dp", None),
        P(None, ("dp", "tensor")),
        P(None, ("dp", "tensor")),
        P(("dp", "tensor"), None),
    )
    body = functools.partial(local, mesh.shape["dp"], mesh.shape["tensor"])
    return jax.shard_map(
        body, mesh=mesh, in_specs=in_specs, out_specs=P(("dp", "tensor"), None), check_vma=False
    )
```

profile of v0, /device:TPU:0, one launch (start us, length us, event | category | flops | bytes accessed | tf_op | source)
XLA Modules:
  0.0 51.2 jit_solution(10454954748279445544)
XLA Ops:
  0.0 1.4 %copy.13.ids = s32[16,2]{1,0:T(8,128)} copy(s32[16,2]{0,1:T(2,128)} %param.14) | data formatting | bytes 256 | tf_op args[2]
  1.4 1.3 %copy.14.route = f32[16,2]{1,0:T(8,128)} copy(f32[16,2]{0,1:T(2,128)} %param.15) | data formatting | bytes 256 | tf_op args[3]
  2.7 47.1 %shard_map.118 = bf16[4,4096]{1,0:T(4,128)(2,1)} custom-call(bf16[4,4096]{1,0:T(4,128)(2,1)} %hidden.1, bf16[16,4096]{1,0:T(8,128)(2,1)} %shortcut.1, s32[16,2]{1,0:T(8,128)} %copy.13.ids, f32[16,2]{1,0:T(8,128)} %copy.14.route, f32[1,4096]{1,0:T(1,128)} %bitcast.2, f32[1,4096]{1,0:T(1,128)} %bitcast.3, bf16[4096,1024]{1,0:T(8,128)(2,1)} %dg.1, ...), custom_call_target="tpu_custom_call" | custom-call | tf_op jit(solution)/shard_map/pallas_call | solution.py:345
  49.8 1.4 %copy.16 = bf16[4,4096]{1,0:T(4,128)(2,1)} copy(bf16[4,4096]{1,0:T(4,128)(2,1)} %shard_map.118) | data formatting | bytes 65536
where the time goes:
time: 51.4 us; the launch traced here: 51.2 us
  Pallas kernels  47.1 us (92%)
  local copies, waits for them, and re-layouts  4.08 us (8%)
    pallas_call x1, Pallas kernels, local(): pl.pallas_call(functools.partial(kernel, cfg), out_shape=jax.ShapeDtypeSt...  47.1 us
    unnamed x3, local copies, waits for them, and re-layouts  4.08 us

commit v1 on v0

v1 whole, which is shorter than its diff:
```python
import functools

import jax
import jax.numpy as jnp
from jax import lax
from jax.experimental import pallas as pl
from jax.experimental.pallas import tpu as pltpu
from jax.sharding import PartitionSpec as P

E = 8
TOP = 2
CAP = 6
CP = 8
NQ = 2
EPSILON = 1e-05
MESH = pl.DeviceIdType.MESH
F32 = jnp.float32
BF16 = jnp.bfloat16


def rms_scale(values):
    return lax.rsqrt(jnp.mean(values * values, axis=-1, keepdims=True) + EPSILON)


def each(lo, hi, body):
    if hi - lo <= 8:
        for k in range(lo, hi):
            body(k)
    else:
        def step(k, _):
            body(k)
            return 0

        lax.fori_loop(lo, hi, step, 0)


def silu_mul(g, v):
    return (g / (1.0 + jnp.exp(-g)) * v).astype(BF16)


def kernel(
    cfg,
    hidden, shortcut, ids, route, dgain, mgain, dg, dl, dd, eg, el, ed,
    out,
    pool, epool, dgp, dlp, ddp,
    disp, land, xe, accg, accl, inner_e,
    ag, stage, xd, inner_d, own, part, pland, ds, dland,
    rs, rsland, ret, retland, fin, finland,
    wsem, esem, dsem,
    di_s, di_r, pd_s, pd_r, ag_s, ag_r, px_s, px_r,
    pr_s, pr_r, re_s, re_r, po_s, po_r, ds_s, ds_r, fi_s, fi_r,
):
    np_, nt, sp, reuse = cfg
    h, D = hidden.shape
    B = shortcut.shape[0]
    fe = eg.shape[1]
    fd = dg.shape[1] // sp
    Dh = D // 2
    kc = Dh // NQ
    nk = 2 * NQ
    dc = D // 2
    members = np_ // E
    rows = np_ * CP
    p = lax.axis_index("dp")
    t = lax.axis_index("tensor")
    c = lax.rem(t, 2)
    mate = t + 1 - 2 * c

    def half(k):
        return c if k < NQ else 1 - c

    def k_rows(k):
        return pl.ds(pl.multiple_of(half(k) * Dh + (k % NQ) * kc, kc), kc)

    def w_copy(k, which):
        src = (eg, el)[which]
        return pltpu.make_async_copy(src.at[k_rows(k), :], pool.at[2 * k + which], wsem.at[2 * k + which])

    def e_cols(i):
        side = 1 - c if i < NQ else c
        return pl.ds(pl.multiple_of(side * Dh + (i % NQ) * kc, kc), kc)

    def e_copy(i):
        return pltpu.make_async_copy(ed.at[:, e_cols(i)], epool.at[i], esem.at[i])

    dcols = pl.ds(pl.multiple_of((c if sp == 2 else 0) * fd, fd), fd)

    def dense_w(k, which):
        if reuse:
            return pool.at[which, :, k * fd : (k + 1) * fd]
        return (dgp, dlp)[which].at[k]

    def dense_d(i):
        if reuse:
            return pool.at[2, i * fd : (i + 1) * fd, :]
        return ddp.at[i]

    def d_copy(k, which):
        src = (dg, dl)[which]
        return pltpu.make_async_copy(
            src.at[k * kc : (k + 1) * kc, dcols], dense_w(k, which), dsem.at[2 * k + which]
        )

    def dd_copy(i):
        return pltpu.make_async_copy(
            dd.at[dcols, i * dc : (i + 1) * dc], dense_d(i), dsem.at[2 * nk + i]
        )

    barrier = pltpu.get_barrier_semaphore()
    land[...] = jnp.zeros(land.shape, BF16)
    retland[...] = jnp.zeros(retland.shape, BF16)

    def greet(k):
        pl.semaphore_signal(
            barrier, inc=1, device_id=(lax.rem(p + k, np_), t), device_id_type=MESH
        )

    each(1, np_, greet)
    for j in range(1, nt):
        pl.semaphore_signal(
            barrier, inc=1, device_id=(p, lax.rem(t + j, nt)), device_id_type=MESH
        )

    for k in range(nk):
        w_copy(k, 0).start()
        w_copy(k, 1).start()
    for i in range(nk):
        e_copy(i).start()
    if not reuse:
        for k in range(nk):
            d_copy(k, 0).start()
            d_copy(k, 1).start()
        for i in range(2):
            dd_copy(i).start()

    wide = np_ * CP
    col = lax.broadcasted_iota(jnp.int32, (B, max(wide, 128)), 1)

    def places(members):
        col_e = lax.shift_right_logical(col, 3) // members
        at0 = jnp.where(ids[:, 0:1] == col_e, 1.0, 0.0).astype(F32)
        at1 = jnp.where(ids[:, 1:2] == col_e, 1.0, 0.0).astype(F32)
        return at0, at1

    r_i = lax.broadcasted_iota(jnp.int32, (B, B), 0)
    c_i = lax.broadcasted_iota(jnp.int32, (B, B), 1)
    lower = jnp.where(c_i < r_i, 1.0, 0.0).astype(BF16)

    def spread_of(members):
        at0, at1 = places(members)
        named = at0 + at1
        before = jnp.dot(lower, named.astype(BF16), preferred_element_type=F32)
        spread = jnp.where(before.astype(jnp.int32) == (col & 7), named, 0.0)
        return spread, at0, at1

    spread = spread_of(1)[0]
    spread_t = jnp.transpose(spread)[: E * CP].astype(BF16)

    sc = rms_scale(shortcut[...].astype(F32))
    for q in range(NQ):
        mine = pl.ds(pl.multiple_of(c * Dh + q * kc, kc), kc)
        moe_q = (shortcut[:, mine].astype(F32) * sc * mgain[:, mine]).astype(BF16)
        buf = jnp.dot(spread_t, moe_q, preferred_element_type=F32)
        disp[q] = buf.reshape(E, CP, kc).astype(BF16)

    hid = hidden[...].astype(F32)
    ag[p] = (hid * rms_scale(hid) * dgain[...]).astype(BF16)

    real = pl.ds(0, CAP)

    def di_copy(k, q, src):
        to = lax.rem(p + k, np_)
        return pltpu.make_async_remote_copy(
            src_ref=disp.at[q, to // members, real], dst_ref=land.at[c, q, src, real],
            send_sem=di_s.at[q, k], recv_sem=di_r.at[q, src], device_id=(to, t),
            device_id_type=MESH,
        )

    def ag_copy(k, src):
        return pltpu.make_async_remote_copy(
            src_ref=ag.at[src], dst_ref=ag.at[src], send_sem=ag_s.at[k],
            recv_sem=ag_r.at[src], device_id=(lax.rem(p + k, np_), t), device_id_type=MESH,
        )

    def mate_copy(src, dst, send, recv):
        return pltpu.make_async_remote_copy(
            src_ref=src, dst_ref=dst, send_sem=send, recv_sem=recv, device_id=(p, mate),
            device_id_type=MESH,
        )

    pl.semaphore_wait(barrier, np_ + nt - 2)
    for q in range(NQ):
        each(1, np_, lambda k: di_copy(k, q, p).start())
    each(1, np_, lambda k: ag_copy(k, p).start())

    for q in range(NQ):
        land[c, q, p] = disp[q, p // members]

    spread_m, at0, at1 = spread_of(members)
    weighted = spread_m * (at0 * route[:, 0:1] + at1 * route[:, 1:2])
    weighted = weighted[:, :wide]
    w_hi = weighted.astype(BF16)
    w_lo = (weighted - w_hi.astype(F32)).astype(BF16)

    def pd_copy(q, side):
        return mate_copy(land.at[side, q], land.at[side, q], pd_s.at[q], pd_r.at[q])

    nb = max(fe // 512, 1)
    cb = fe // nb
    for k in range(nk):
        q = k % NQ
        if k < NQ:
            each(1, np_, lambda j: di_copy(j, q, lax.rem(p + j, np_)).wait_recv())
            pd_copy(q, c).start()
        else:
            pd_copy(q, 1 - c).wait_recv()
        xe[k] = land[half(k), q].astype(F32).reshape(rows, kc).astype(BF16)
        w_copy(k, 0).wait()
        w_copy(k, 1).wait()
        if k == 0:
            accg[...] = jnp.dot(xe[k], pool[0], preferred_element_type=F32)
            accl[...] = jnp.dot(xe[k], pool[1], preferred_element_type=F32)
        elif k < nk - 1:
            accg[...] = accg[...] + jnp.dot(xe[k], pool[2 * k], preferred_element_type=F32)
            accl[...] = accl[...] + jnp.dot(xe[k], pool[2 * k + 1], preferred_element_type=F32)
        else:
            for b in range(nb):
                cols = slice(b * cb, (b + 1) * cb)
                g = accg[:, cols] + jnp.dot(xe[k], pool[2 * k, :, cols], preferred_element_type=F32)
                v = accl[:, cols] + jnp.dot(xe[k], pool[2 * k + 1, :, cols], preferred_element_type=F32)
                inner_e[:, cols] = silu_mul(g, v)
        if reuse and k == 0:
            for i in range(nk):
                d_copy(i, 0).start()
                d_copy(i, 1).start()
        if reuse and k == 1:
            for i in range(2):
                dd_copy(i).start()

    nh = np_ * h
    me = c if sp == 2 else 0
    each(1, np_, lambda k: ag_copy(k, lax.rem(p + k, np_)).wait_recv())
    for s in range(np_):
        stage[s * h : (s + 1) * h, :] = ag[s].astype(F32)
    xd[me] = stage[...].astype(BF16)
    if sp == 2:
        px = mate_copy(xd.at[me], xd.at[me], px_s.at[0], px_r.at[0])
        px.start()

    def pr_copy(q):
        return mate_copy(rs.at[q], rsland.at[q], pr_s.at[q], pr_r.at[q])

    def re_copy(k, q, src):
        to = lax.rem(p + k, np_)
        return pltpu.make_async_remote_copy(
            src_ref=ret.at[q, to, real], dst_ref=retland.at[q, src, real],
            send_sem=re_s.at[q, k], recv_sem=re_r.at[q, src], device_id=(to, t),
            device_id_type=MESH,
        )

    for i in range(nk):
        q = i % NQ
        e_copy(i).wait()
        o = jnp.dot(inner_e[...], epool[i], preferred_element_type=F32)
        if i < NQ:
            rs[q] = o.reshape(np_, CP, kc).astype(BF16)
            pr_copy(q).start()
        else:
            pr_copy(q).wait_recv()
            ret[q] = (o.reshape(np_, CP, kc) + rsland[q].astype(F32)).astype(BF16)
            each(1, np_, lambda k: re_copy(k, q, p).start())
            retland[q, p] = ret[q, p]

    if sp == 2:
        mate_copy(xd.at[1 - me], xd.at[1 - me], px_s.at[0], px_r.at[0]).wait_recv()
    g = None
    for k in range(nk):
        d_copy(k, 0).wait()
        d_copy(k, 1).wait()
    xk = xd[...].astype(F32).reshape(sp * nh, D).astype(BF16)
    g = v = None
    for k in range(nk):
        lhs = xk[:, k * kc : (k + 1) * kc]
        gk = jnp.dot(lhs, dense_w(k, 0)[...], preferred_element_type=F32)
        vk = jnp.dot(lhs, dense_w(k, 1)[...], preferred_element_type=F32)
        g = gk if g is None else g + gk
        v = vk if v is None else v + vk
    inner_d[...] = silu_mul(g, v)

    def po_copy(i):
        return mate_copy(part.at[i], pland.at[i], po_s.at[i], po_r.at[i])

    def ds_copy(k, i, src):
        to = lax.rem(p + k, np_)
        return pltpu.make_async_remote_copy(
            src_ref=ds.at[i, to], dst_ref=dland.at[i, src], send_sem=ds_s.at[i, k],
            recv_sem=ds_r.at[i, src], device_id=(to, t), device_id_type=MESH,
        )

    for i in range(2):
        dd_copy(i).wait()
        o = jnp.dot(inner_d[...], dense_d(i)[...], preferred_element_type=F32)
        if sp == 2:
            own[i] = jnp.where(c == 0, o[:nh], o[nh:])
            part[i] = jnp.where(c == 0, o[nh:], o[:nh]).astype(BF16)
            po_copy(i).start()
        else:
            own[i] = o
    for i in range(2):
        o = own[i]
        if sp == 2:
            po_copy(i).wait_recv()
            o = o + pland[i].astype(F32)
        for s in range(np_):
            ds[i, s] = o[s * h : (s + 1) * h, :].astype(BF16)
        each(1, np_, lambda k: ds_copy(k, i, p).start())
        dland[i, p] = ds[i, p]

    def fi_copy(j, q, src):
        to = lax.rem(t + j, nt)
        return pltpu.make_async_remote_copy(
            src_ref=fin.at[to, q], dst_ref=finland.at[src, q], send_sem=fi_s.at[j, q],
            recv_sem=fi_r.at[src, q], device_id=(p, to), device_id_type=MESH,
        )

    for q in range(NQ):
        each(1, np_, lambda k: re_copy(k, q, lax.rem(p + k, np_)).wait_recv())
        back = retland[q].astype(F32).reshape(rows, kc).astype(BF16)
        moe = jnp.dot(w_hi, back, preferred_element_type=F32)
        moe = moe + jnp.dot(w_lo, back, preferred_element_type=F32)
        for j in range(nt):
            fin[j, q] = moe[j * h : (j + 1) * h, :].astype(BF16)
        for j in range(1, nt):
            fi_copy(j, q, t).start()
        finland[t, q] = fin[t, q]

    for i in range(2):
        each(1, np_, lambda k: ds_copy(k, i, lax.rem(p + k, np_)).wait_recv())
    for q in range(NQ):
        for j in range(1, nt):
            fi_copy(j, q, lax.rem(t + j, nt)).wait_recv()
    for i in range(2):
        acc = hid[:, i * dc : (i + 1) * dc]
        for s in range(np_):
            acc = acc + dland[i, s].astype(F32)
        for q in range(NQ):
            a = acc[:, q * kc : (q + 1) * kc]
            for j in range(i, nt, 2):
                a = a + finland[j, q].astype(F32)
            out[:, i * Dh + q * kc : i * Dh + (q + 1) * kc] = a.astype(BF16)

    def sent(k):
        for q in range(NQ):
            di_copy(k, q, p).wait_send()
            re_copy(k, q, p).wait_send()
        ag_copy(k, p).wait_send()
        for i in range(2):
            ds_copy(k, i, p).wait_send()

    each(1, np_, sent)
    for q in range(NQ):
        pd_copy(q, c).wait_send()
        pr_copy(q).wait_send()
        for j in range(1, nt):
            fi_copy(j, q, t).wait_send()
    if sp == 2:
        px.wait_send()
        for i in range(2):
            po_copy(i).wait_send()


def local(np_, nt, hidden, shortcut, ids, route, dgain, mgain, dg, dl, dd, eg, el, ed):
    h, D = hidden.shape
    fe = eg.shape[1]
    sp = 2 if dg.shape[1] % 256 == 0 else 1
    fd = dg.shape[1] // sp
    Dh = D // 2
    kc = Dh // NQ
    nk = 2 * NQ
    reuse = nk * fd <= fe and Dh <= fe and 2 * fd <= kc
    nh = np_ * h
    rows = np_ * CP
    dma = pltpu.SemaphoreType.DMA
    vm = pltpu.VMEM
    vspec = pl.BlockSpec(memory_space=pltpu.VMEM)
    aspec = pl.BlockSpec(memory_space=pl.ANY)
    tiny = vm((8, 128), BF16)
    return pl.pallas_call(
        functools.partial(kernel, (np_, nt, sp, reuse)),
        out_shape=jax.ShapeDtypeStruct((h, D), BF16),
        in_specs=[vspec] * 6 + [aspec] * 6,
        out_specs=vspec,
        scratch_shapes=[
            vm((2 * nk, kc, fe), BF16), vm((nk, fe, kc), BF16),
            tiny if reuse else vm((nk, kc, fd), BF16),
            tiny if reuse else vm((nk, kc, fd), BF16),
            tiny if reuse else vm((2, fd, Dh), BF16),
            vm((NQ, E, CP, kc), BF16), vm((2, NQ, np_, CP, kc), BF16), vm((nk, rows, kc), BF16),
            vm((rows, fe), F32), vm((rows, fe), F32), vm((rows, fe), BF16),
            vm((np_, h, D), BF16), vm((nh, D), F32), vm((sp, nh, D), BF16), vm((sp * nh, fd), BF16),
            vm((2, nh, Dh), F32), vm((2, nh, Dh), BF16), vm((2, nh, Dh), BF16),
            vm((2, np_, h, Dh), BF16), vm((2, np_, h, Dh), BF16),
            vm((NQ, np_, CP, kc), BF16), vm((NQ, np_, CP, kc), BF16),
            vm((NQ, np_, CP, kc), BF16), vm((NQ, np_, CP, kc), BF16),
            vm((nt, NQ, h, kc), BF16), vm((nt, NQ, h, kc), BF16),
            dma((2 * nk,)), dma((nk,)), dma((2 * nk + 2,)),
            dma((NQ, np_)), dma((NQ, np_)), dma((NQ,)), dma((NQ,)), dma((np_,)), dma((np_,)),
            dma((1,)), dma((1,)),
            dma((NQ,)), dma((NQ,)), dma((NQ, np_)), dma((NQ, np_)), dma((2,)), dma((2,)),
            dma((2, np_)), dma((2, np_)), dma((nt, NQ)), dma((nt, NQ)),
        ],
        compiler_params=pltpu.CompilerParams(
            collective_id=0, has_side_effects=True, vmem_limit_bytes=64 * 1024 * 1024 - 65536
        ),
    )(hidden, shortcut, ids, route, dgain.reshape(1, D), mgain.reshape(1, D), dg, dl, dd, eg, el, ed)


def solution(mesh):
    in_specs = (
        P(("dp", "tensor"), None),
        P("dp", None),
        P("dp", None),
        P("dp", None),
        P(),
        P(),
        P(None, "dp"),
        P(None, "dp"),
        P("dp", None),
        P(None, ("dp", "tensor")),
        P(None, ("dp", "tensor")),
        P(("dp", "tensor"), None),
    )
    body = functools.partial(local, mesh.shape["dp"], mesh.shape["tensor"])
    return jax.shard_map(
        body, mesh=mesh, in_specs=in_specs, out_specs=P(("dp", "tensor"), None), check_vma=False
    )
```

time: 51.4 us -> 40.2 us (0.78)
  Pallas kernels: 47.1 us -> 35.9 us
    pallas_call x1, Pallas kernels: 47.1 us -> 35.9 us  [local(): pl.pallas_call(functools.partial(kernel, (np_, nt, sp, reuse)), out_shape...]
where the time goes in v1:
time: 40.2 us; the launch traced here: 40 us
  Pallas kernels  35.9 us (89%)
  local copies, waits for them, and re-layouts  4.08 us (10%)
    pallas_call x1, Pallas kernels, local(): pl.pallas_call(functools.partial(kernel, (np_, nt, sp, reuse)), out_shape...  35.9 us
    unnamed x3, local copies, waits for them, and re-layouts  4.08 us

profile of v1, /device:TPU:0, one launch (start us, length us, event | category | flops | bytes accessed | tf_op | source)
XLA Modules:
  0.0 40.0 jit_solution(2719834822129629582)
XLA Ops:
  0.0 1.4 %copy.13.ids = s32[16,2]{1,0:T(8,128)} copy(s32[16,2]{0,1:T(2,128)} %param.14) | data formatting | bytes 256 | tf_op args[2]
  1.4 1.3 %copy.14.route = f32[16,2]{1,0:T(8,128)} copy(f32[16,2]{0,1:T(2,128)} %param.15) | data formatting | bytes 256 | tf_op args[3]
  2.7 35.9 %shard_map.118 = bf16[4,4096]{1,0:T(4,128)(2,1)} custom-call(bf16[4,4096]{1,0:T(4,128)(2,1)} %hidden.1, bf16[16,4096]{1,0:T(8,128)(2,1)} %shortcut.1, s32[16,2]{1,0:T(8,128)} %copy.13.ids, f32[16,2]{1,0:T(8,128)} %copy.14.route, f32[1,4096]{1,0:T(1,128)} %bitcast.2, f32[1,4096]{1,0:T(1,128)} %bitcast.3, bf16[4096,1024]{1,0:T(8,128)(2,1)} %dg.1, ...), custom_call_target="tpu_custom_call" | custom-call | tf_op jit(solution)/shard_map/pallas_call | solution.py:388
  38.6 1.4 %copy.16 = bf16[4,4096]{1,0:T(4,128)(2,1)} copy(bf16[4,4096]{1,0:T(4,128)(2,1)} %shard_map.118) | data formatting | bytes 65536

commit v2 on v1

--- a/solution.py
+++ b/solution.py
@@ -40,13 +40,14 @@
 
 def kernel(
     cfg,
-    hidden, shortcut, ids, route, dgain, mgain, dg, dl, dd, eg, el, ed,
+    hidden_, shortcut_, ids_, route_, dgain_, mgain_, dg, dl, dd, eg, el, ed,
     out,
+    hidden, shortcut, ids, route, dgain, mgain,
     pool, epool, dgp, dlp, ddp,
     disp, land, xe, accg, accl, inner_e,
     ag, stage, xd, inner_d, own, part, pland, ds, dland,
     rs, rsland, ret, retland, fin, finland,
-    wsem, esem, dsem,
+    isem, wsem, esem, dsem,
     di_s, di_r, pd_s, pd_r, ag_s, ag_r, px_s, px_r,
     pr_s, pr_r, re_s, re_r, po_s, po_r, ds_s, ds_r, fi_s, fi_r,
 ):
@@ -106,6 +107,12 @@
             dd.at[dcols, i * dc : (i + 1) * dc], dense_d(i), dsem.at[2 * nk + i]
         )
 
+    small = (
+        (ids_, ids), (route_, route), (mgain_, mgain), (shortcut_, shortcut), (hidden_, hidden), (dgain_, dgain)
+    )
+    small = [pltpu.make_async_copy(a, b, isem.at[i]) for i, (a, b) in enumerate(small)]
+    for copy in small:
+        copy.start()
     barrier = pltpu.get_barrier_semaphore()
     land[...] = jnp.zeros(land.shape, BF16)
     retland[...] = jnp.zeros(retland.shape, BF16)
@@ -133,28 +140,22 @@
         for i in range(2):
             dd_copy(i).start()
 
-    wide = np_ * CP
-    col = lax.broadcasted_iota(jnp.int32, (B, max(wide, 128)), 1)
-
-    def places(members):
-        col_e = lax.shift_right_logical(col, 3) // members
-        at0 = jnp.where(ids[:, 0:1] == col_e, 1.0, 0.0).astype(F32)
-        at1 = jnp.where(ids[:, 1:2] == col_e, 1.0, 0.0).astype(F32)
-        return at0, at1
-
+    for copy in small:
+        copy.wait()
     r_i = lax.broadcasted_iota(jnp.int32, (B, B), 0)
     c_i = lax.broadcasted_iota(jnp.int32, (B, B), 1)
-    lower = jnp.where(c_i < r_i, 1.0, 0.0).astype(BF16)
-
-    def spread_of(members):
-        at0, at1 = places(members)
+    earlier = jnp.where(r_i < c_i, 1.0, 0.0).astype(BF16)
+
+    def spread_of(n, members):
+        row = lax.broadcasted_iota(jnp.int32, (n, B), 0)
+        row_e = lax.shift_right_logical(row, 3) // members
+        at0 = jnp.where(ids[0:1, :] == row_e, 1.0, 0.0).astype(F32)
+        at1 = jnp.where(ids[1:2, :] == row_e, 1.0, 0.0).astype(F32)
         named = at0 + at1
-        before = jnp.dot(lower, named.astype(BF16), preferred_element_type=F32)
-        spread = jnp.where(before.astype(jnp.int32) == (col & 7), named, 0.0)
-        return spread, at0, at1
-
-    spread = spread_of(1)[0]
-    spread_t = jnp.transpose(spread)[: E * CP].astype(BF16)
+        before = jnp.dot(named.astype(BF16), earlier, preferred_element_type=F32)
+        return jnp.where(before.astype(jnp.int32) == (row & 7), named, 0.0), at0, at1
+
+    spread_t = spread_of(E * CP, 1)[0].astype(BF16)
 
     sc = rms_scale(shortcut[...].astype(F32))
     for q in range(NQ):
@@ -196,11 +197,13 @@
     for q in range(NQ):
         land[c, q, p] = disp[q, p // members]
 
-    spread_m, at0, at1 = spread_of(members)
-    weighted = spread_m * (at0 * route[:, 0:1] + at1 * route[:, 1:2])
-    weighted = weighted[:, :wide]
+    spread_m, at0, at1 = spread_of(rows, members)
+    weighted = spread_m * (at0 * route[0:1, :] + at1 * route[1:2, :])
     w_hi = weighted.astype(BF16)
     w_lo = (weighted - w_hi.astype(F32)).astype(BF16)
+
+    def spread_back(w, x):
+        return lax.dot_general(w, x, (((0,), (0,)), ((), ())), preferred_element_type=F32)
 
     def pd_copy(q, side):
         return mate_copy(land.at[side, q], land.at[side, q], pd_s.at[q], pd_r.at[q])
@@ -242,9 +245,11 @@
     each(1, np_, lambda k: ag_copy(k, lax.rem(p + k, np_)).wait_recv())
     for s in range(np_):
         stage[s * h : (s + 1) * h, :] = ag[s].astype(F32)
-    xd[me] = stage[...].astype(BF16)
+    mine = pl.ds(pl.multiple_of(me * nh, nh), nh)
+    theirs = pl.ds(pl.multiple_of((sp - 1 - me) * nh, nh), nh)
+    xd[mine, :] = stage[...].astype(BF16)
     if sp == 2:
-        px = mate_copy(xd.at[me], xd.at[me], px_s.at[0], px_r.at[0])
+        px = mate_copy(xd.at[mine], xd.at[mine], px_s.at[0], px_r.at[0])
         px.start()
 
     def pr_copy(q):
@@ -272,15 +277,13 @@
             retland[q, p] = ret[q, p]
 
     if sp == 2:
-        mate_copy(xd.at[1 - me], xd.at[1 - me], px_s.at[0], px_r.at[0]).wait_recv()
-    g = None
+        mate_copy(xd.at[theirs], xd.at[theirs], px_s.at[0], px_r.at[0]).wait_recv()
     for k in range(nk):
         d_copy(k, 0).wait()
         d_copy(k, 1).wait()
-    xk = xd[...].astype(F32).reshape(sp * nh, D).astype(BF16)
     g = v = None
     for k in range(nk):
-        lhs = xk[:, k * kc : (k + 1) * kc]
+        lhs = xd[:, k * kc : (k + 1) * kc]
         gk = jnp.dot(lhs, dense_w(k, 0)[...], preferred_element_type=F32)
         vk = jnp.dot(lhs, dense_w(k, 1)[...], preferred_element_type=F32)
         g = gk if g is None else g + gk
@@ -326,8 +329,7 @@
     for q in range(NQ):
         each(1, np_, lambda k: re_copy(k, q, lax.rem(p + k, np_)).wait_recv())
         back = retland[q].astype(F32).reshape(rows, kc).astype(BF16)
-        moe = jnp.dot(w_hi, back, preferred_element_type=F32)
-        moe = moe + jnp.dot(w_lo, back, preferred_element_type=F32)
+        moe = spread_back(w_hi, back) + spread_back(w_lo, back)
         for j in range(nt):
             fin[j, q] = moe[j * h : (j + 1) * h, :].astype(BF16)
         for j in range(1, nt):
@@ -371,6 +373,7 @@
 
 def local(np_, nt, hidden, shortcut, ids, route, dgain, mgain, dg, dl, dd, eg, el, ed):
     h, D = hidden.shape
+    B = shortcut.shape[0]
     fe = eg.shape[1]
     sp = 2 if dg.shape[1] % 256 == 0 else 1
     fd = dg.shape[1] // sp
@@ -387,32 +390,34 @@
     tiny = vm((8, 128), BF16)
     return pl.pallas_call(
         functools.partial(kernel, (np_, nt, sp, reuse)),
-        out_shape=jax.ShapeDtypeStruct((h, D), BF16),
-        in_specs=[vspec] * 6 + [aspec] * 6,
+        out_shape=pltpu.VMEM((h, D), BF16),
+        in_specs=[aspec] * 12,
         out_specs=vspec,
         scratch_shapes=[
+            vm((h, D), BF16), vm((B, D), BF16), vm((TOP, B), jnp.int32), vm((TOP, B), F32),
+            vm((1, D), F32), vm((1, D), F32),
             vm((2 * nk, kc, fe), BF16), vm((nk, fe, kc), BF16),
             tiny if reuse else vm((nk, kc, fd), BF16),
             tiny if reuse else vm((nk, kc, fd), BF16),
             tiny if reuse else vm((2, fd, Dh), BF16),
             vm((NQ, E, CP, kc), BF16), vm((2, NQ, np_, CP, kc), BF16), vm((nk, rows, kc), BF16),
             vm((rows, fe), F32), vm((rows, fe), F32), vm((rows, fe), BF16),
-            vm((np_, h, D), BF16), vm((nh, D), F32), vm((sp, nh, D), BF16), vm((sp * nh, fd), BF16),
+            vm((np_, h, D), BF16), vm((nh, D), F32), vm((sp * nh, D), BF16), vm((sp * nh, fd), BF16),
             vm((2, nh, Dh), F32), vm((2, nh, Dh), BF16), vm((2, nh, Dh), BF16),
             vm((2, np_, h, Dh), BF16), vm((2, np_, h, Dh), BF16),
             vm((NQ, np_, CP, kc), BF16), vm((NQ, np_, CP, kc), BF16),
             vm((NQ, np_, CP, kc), BF16), vm((NQ, np_, CP, kc), BF16),
             vm((nt, NQ, h, kc), BF16), vm((nt, NQ, h, kc), BF16),
-            dma((2 * nk,)), dma((nk,)), dma((2 * nk + 2,)),
+            dma((6,)), dma((2 * nk,)), dma((nk,)), dma((2 * nk + 2,)),
             dma((NQ, np_)), dma((NQ, np_)), dma((NQ,)), dma((NQ,)), dma((np_,)), dma((np_,)),
             dma((1,)), dma((1,)),
             dma((NQ,)), dma((NQ,)), dma((NQ, np_)), dma((NQ, np_)), dma((2,)), dma((2,)),
             dma((2, np_)), dma((2, np_)), dma((nt, NQ)), dma((nt, NQ)),
         ],
         compiler_params=pltpu.CompilerParams(
-            collective_id=0, has_side_effects=True, vmem_limit_bytes=64 * 1024 * 1024 - 65536
+            collective_id=0, has_side_effects=True, vmem_limit_bytes=64 * 1024 * 1024 - 262144
         ),
-    )(hidden, shortcut, ids, route, dgain.reshape(1, D), mgain.reshape(1, D), dg, dl, dd, eg, el, ed)
+    )(hidden, shortcut, ids.T, route.T, dgain.reshape(1, D), mgain.reshape(1, D), dg, dl, dd, eg, el, ed)
 
 
 def solution(mesh):

time: 40.2 us -> 34.9 us (0.87)
  local copies, waits for them, and re-layouts: 4.08 us -> 0.62 us
  Pallas kernels: 35.9 us -> 34.2 us
    unnamed x3 -> x1, local copies, waits for them, and re-layouts: 4.08 us -> 0.62 us
    pallas_call x1, Pallas kernels: 35.9 us -> 34.2 us  [local(): pl.pallas_call(functools.partial(kernel, (np_, nt, sp, reuse)), out_shape...]
where the time goes in v2:
time: 34.9 us; the launch traced here: 34.8 us
  Pallas kernels  34.2 us (98%)
  local copies, waits for them, and re-layouts  0.62 us (2%)
    pallas_call x1, Pallas kernels, local(): pl.pallas_call(functools.partial(kernel, (np_, nt, sp, reuse)), out_shape...  34.2 us

profile of v2, /device:TPU:0, one launch (start us, length us, event | category | flops | bytes accessed | tf_op | source)
XLA Modules:
  0.0 34.8 jit_solution(13808214871441359990)
XLA Ops:
  0.0 34.2 %shard_map.118 = bf16[4,4096]{1,0:T(4,128)(2,1)S(1)} custom-call(bf16[4,4096]{1,0:T(4,128)(2,1)} %hidden_.1, bf16[16,4096]{1,0:T(8,128)(2,1)} %shortcut_.1, s32[2,16]{1,0:T(2,128)} %bitcast.6, f32[2,16]{1,0:T(2,128)} %bitcast.7, f32[1,4096]{1,0:T(1,128)} %bitcast.4, f32[1,4096]{1,0:T(1,128)} %bitcast.5, bf16[4096,1024]{1,0:T(8,128)(2,1)} %dg.1, ...), custom_call_target="tpu_custom_call" | custom-call | tf_op jit(solution)/shard_map/pallas_call | solution.py:391
  34.2 0.6 %copy.14 = bf16[4,4096]{1,0:T(4,128)(2,1)} copy(bf16[4,4096]{1,0:T(4,128)(2,1)S(1)} %shard_map.118) | data formatting | bytes 65536
